TPU v7x, 1024 devices: a whole 4x8x16 slice. The times are simulated.
1024 devices in a mesh: face: 16 (over z_hi, x), tile: 16 (over y, core), lev: 4 (over z_lo).
Axes of the slice: x: 4, y: 8, z: 16 (z_hi: 4, z_lo: 4; z = z_hi * 4 + z_lo), core: 2. Of those that a mesh axis runs over, the one named last changes fastest.
Arguments:
- airflow_components: float32 [2, 72, 128, 2048], P(None, 'lev', 'face', 'tile'), may hold values from -4.5 to 4.5, as said below
- heat_state: float32 [72, 128, 2048], P('lev', 'face', 'tile'), may hold values from 0.5 to 2
- layer_pressure_depth: float32 [72, 128, 2048], P('lev', 'face', 'tile'), may hold values from 0.5 to 2
- constituent_masses: float32 [18, 72, 128, 2048], P(None, 'lev', 'face', 'tile'), may hold values from 0.1 to 1
- ground_gravity_potential: float32 [128, 2048], P('face', 'tile'), may hold values from -8 to 8
- inverse_mapping_entries: float32 [4, 128, 2048], P(None, 'face', 'tile'), may hold values from -4 to 4
- mapping_determinant: float32 [128, 2048], P('face', 'tile'), may hold values from 0.5 to 2
- interface_rightangle_rotations: int32 [16, 16, 2], replicated, may hold values from 0 to 3
- interface_flipped_markers: int32 [16, 16, 2], replicated, may hold values from 0 to 1
- corner_block_tally: int32 [16, 16], replicated, may hold values from 3 to 4
Outputs:
- airflow_next: float32 [2, 72, 128, 2048], P(None, 'lev', 'face', 'tile')
- heat_state_next: float32 [72, 128, 2048], P('lev', 'face', 'tile')
- pressure_depth_next: float32 [72, 128, 2048], P('lev', 'face', 'tile')
- constituent_masses_next: float32 [18, 72, 128, 2048], P(None, 'lev', 'face', 'tile')
- stepping_bounds: float32 [2], replicated
Inputs may be any that keep to these rules, and one draw needn't show every extreme that they name: `airflow_components`: component magnitudes grow across the grid by up to a factor of 9. `interface_rightangle_rotations`: entry [f, t, 0] concerns the boundary between blocks (f, t) and (f+1, t), entry [f, t, 1] the one between (f, t) and (f, t+1). `interface_flipped_markers`: indexed like interface_rightangle_rotations. `corner_block_tally`: entry [f, t] belongs to the corner shared by blocks (f, t), (f+1, t), (f, t+1), (f+1, t+1).
All inputs are finite; a program needn't handle non-finite values.
Results may differ from a plain program's by a relative error of at most 0.00012.
Values sent between devices are 32-bit elements; how exact they have to be, the bound alone decides.
No kernel may reach another device: no remote copies, remote signals or barrier semaphores. Data moves between devices by JAX's collectives and lax.ppermute only.
A program may use at most 32 MiB of HBM per device.

v0:
```python
import functools
import math

import jax
import jax.numpy as jnp
import numpy as np
from jax import lax
from jax.sharding import Mesh
from jax.sharding import PartitionSpec as P

FACE_TILE_LEV = ("face_0", "face_1", "tile_0", "tile_1", "lev")
FACE = ("face_0", "face_1")
TILE = ("tile_0", "tile_1")


time_step = 0.05
viscosity = 0.05
highest = lax.Precision.HIGHEST


def carried_in(part, axis, combine, identity):
    count = lax.axis_size(axis)
    place = lax.axis_index(axis)
    ahead = count - 1 - place
    gathered = lax.all_gather(part, axis)
    state = jnp.zeros_like(part) + jnp.asarray(identity, part.dtype)

    def one(turn, state):
        source = count - 1 - turn
        return combine(state, lax.dynamic_index_in_dim(gathered, source, 0, False))

    return lax.fori_loop(0, ahead, one, state)


def one_axis_at_a_time(x, axes):
    return functools.reduce(lax.pmax, axes, x)


def extended(cells, sides, width):
    for axis, dim in sides:
        count = lax.axis_size(axis)
        head = lax.slice_in_dim(cells, 0, width, axis=dim)
        tail = lax.slice_in_dim(cells, cells.shape[dim] - width, cells.shape[dim], axis=dim)
        cells = jnp.concatenate(
            [
                lax.ppermute(tail, axis, [(i, (i + 1) % count) for i in range(count)]),
                cells,
                lax.ppermute(head, axis, [((i + 1) % count, i) for i in range(count)]),
            ],
            axis=dim,
        )
    return cells


def gll_tables():
    offset = 1.0 / math.sqrt(5.0)
    gll_nodes = np.array([-1.0, -offset, offset, 1.0])
    weights = np.array([1.0 / 6.0, 5.0 / 6.0, 5.0 / 6.0, 1.0 / 6.0])
    barycentric = np.ones(4)
    for outer_index in range(4):
        for inner_index in range(4):
            if inner_index != outer_index:
                barycentric[outer_index] = barycentric[outer_index] / (
                    gll_nodes[outer_index] - gll_nodes[inner_index]
                )
    derivative = np.zeros((4, 4))
    for outer_index in range(4):
        for inner_index in range(4):
            if inner_index != outer_index:
                derivative[outer_index, inner_index] = (
                    barycentric[inner_index]
                    / barycentric[outer_index]
                    / (gll_nodes[outer_index] - gll_nodes[inner_index])
                )
        derivative[outer_index, outer_index] = -np.sum(derivative[outer_index])
    return (derivative, weights)


def advance(
    east_wind,
    north_wind,
    temp_field,
    thick_field,
    tracer_field,
    geo_field,
    inverse_mapping_entries,
    mapping_determinant,
    along_rows,
    along_columns,
):

    def gradient(scalar):
        first_part = along_rows(scalar)
        second_part = along_columns(scalar)
        return (
            inverse_mapping_entries[0] * first_part + inverse_mapping_entries[2] * second_part,
            inverse_mapping_entries[1] * first_part + inverse_mapping_entries[3] * second_part,
        )

    def divergence(east_part, north_part):
        first_flux = mapping_determinant * (
            inverse_mapping_entries[0] * east_part + inverse_mapping_entries[1] * north_part
        )
        second_flux = mapping_determinant * (
            inverse_mapping_entries[2] * east_part + inverse_mapping_entries[3] * north_part
        )
        return (along_rows(first_flux) + along_columns(second_flux)) / mapping_determinant

    energy = 0.5 * (east_wind * east_wind + north_wind * north_wind) + geo_field
    energy_x, energy_y = gradient(energy)
    temp_x, temp_y = gradient(temp_field)
    thick_x, thick_y = gradient(thick_field)
    laplace = divergence(thick_x, thick_y)
    new_east = east_wind - time_step * energy_x
    new_north = north_wind - time_step * energy_y
    new_temp = temp_field - time_step * (east_wind * temp_x + north_wind * temp_y)
    new_thick = (
        thick_field
        - time_step * divergence(thick_field * east_wind, thick_field * north_wind)
        + time_step * viscosity * laplace
    )
    new_tracer = tracer_field - time_step * divergence(
        tracer_field * east_wind, tracer_field * north_wind
    )
    spacing = jnp.sqrt(
        inverse_mapping_entries[0] * inverse_mapping_entries[0]
        + inverse_mapping_entries[1] * inverse_mapping_entries[1]
        + inverse_mapping_entries[2] * inverse_mapping_entries[2]
        + inverse_mapping_entries[3] * inverse_mapping_entries[3]
    )
    courant = jnp.max(
        time_step * jnp.sqrt(east_wind * east_wind + north_wind * north_wind) * spacing
    )
    damping = jnp.max(time_step * viscosity * jnp.abs(laplace))
    fields = jnp.concatenate(
        [new_east[None], new_north[None], new_temp[None], new_thick[None], new_tracer], 0
    )
    return (fields, courant, damping)


def turn(pieces, code):
    cosine = jnp.where(code == 0, 1.0, jnp.where(code == 2, -1.0, 0.0)).astype(jnp.float32)
    sine = jnp.where(code == 1, 1.0, jnp.where(code == 3, -1.0, 0.0)).astype(jnp.float32)
    first_part = cosine * pieces[0] - sine * pieces[1]
    second_part = sine * pieces[0] + cosine * pieces[1]
    return jnp.concatenate([first_part[None], second_part[None], pieces[2:]], 0)


def flip_edge(strip, flag):
    return jnp.where(flag[..., None] == 1, strip[..., ::-1], strip)


def fix_edge(strip, flag, code):
    return turn(flip_edge(strip, flag), code[..., None])


def assemble(
    inner, top_rim, bottom_rim, left_rim, right_rim, corner_ll, corner_lh, corner_hl, corner_hh
):
    first_row = jnp.concatenate([corner_ll[..., None], top_rim, corner_lh[..., None]], -1)
    last_row = jnp.concatenate([corner_hl[..., None], bottom_rim, corner_hh[..., None]], -1)
    middle = jnp.concatenate([left_rim[..., None], inner, right_rim[..., None]], -1)
    return jnp.concatenate([first_row[..., None, :], middle, last_row[..., None, :]], -2)


def shared_sums(padded):
    row_count = padded.shape[-2] - 2
    column_count = padded.shape[-1] - 2
    row_low = (jnp.arange(row_count) % 4 == 0)[:, None]
    row_high = (jnp.arange(row_count) % 4 == 3)[:, None]
    across = (
        padded[..., 1:-1, :]
        + jnp.where(row_low, padded[..., :-2, :], 0.0)
        + jnp.where(row_high, padded[..., 2:, :], 0.0)
    )
    column_low = jnp.arange(column_count) % 4 == 0
    column_high = jnp.arange(column_count) % 4 == 3
    return (
        across[..., 1:-1]
        + jnp.where(column_low, across[..., :-2], 0.0)
        + jnp.where(column_high, across[..., 2:], 0.0)
    )


def combine_block(pieces, mass_pieces, rotations, flips, valences):
    inner, top_rim, bottom_rim, left_rim, right_rim, corner_ll, corner_lh, corner_hl, corner_hh = (
        pieces
    )
    mass_inner, mass_top, mass_bottom, mass_left, mass_right, mass_ll, mass_lh, mass_hl, mass_hh = (
        mass_pieces
    )
    top_code, bottom_code, left_code, right_code = rotations
    top_flag, bottom_flag, left_flag, right_flag = flips
    valence_ll, valence_lh, valence_hl, valence_hh = valences
    fixed = assemble(
        inner,
        fix_edge(top_rim, top_flag, top_code),
        fix_edge(bottom_rim, bottom_flag, bottom_code),
        fix_edge(left_rim, left_flag, left_code),
        fix_edge(right_rim, right_flag, right_code),
        jnp.where(valence_ll == 4, turn(corner_ll, (top_code + left_code) % 4), 0.0),
        jnp.where(valence_lh == 4, turn(corner_lh, (top_code + right_code) % 4), 0.0),
        jnp.where(valence_hl == 4, turn(corner_hl, (bottom_code + left_code) % 4), 0.0),
        jnp.where(valence_hh == 4, turn(corner_hh, (bottom_code + right_code) % 4), 0.0),
    )
    mass_fixed = assemble(
        mass_inner,
        flip_edge(mass_top, top_flag),
        flip_edge(mass_bottom, bottom_flag),
        flip_edge(mass_left, left_flag),
        flip_edge(mass_right, right_flag),
        jnp.where(valence_ll == 4, mass_ll, 0.0),
        jnp.where(valence_lh == 4, mass_lh, 0.0),
        jnp.where(valence_hl == 4, mass_hl, 0.0),
        jnp.where(valence_hh == 4, mass_hh, 0.0),
    )
    return shared_sums(fixed) / shared_sums(mass_fixed)


def rim_pieces(padded):
    return (
        padded[:, :, 1:-1, 1:-1],
        padded[:, :, 0, 1:-1],
        padded[:, :, -1, 1:-1],
        padded[:, :, 1:-1, 0],
        padded[:, :, 1:-1, -1],
        padded[:, :, 0, 0],
        padded[:, :, 0, -1],
        padded[:, :, -1, 0],
        padded[:, :, -1, -1],
    )


def add_terms(earlier, later):
    return earlier + later


def on_device(
    airflow_components,
    heat_state,
    layer_pressure_depth,
    constituent_masses,
    ground_gravity_potential,
    inverse_mapping_entries,
    mapping_determinant,
    interface_rightangle_rotations,
    interface_flipped_markers,
    corner_block_tally,
):
    derivative, weights = gll_tables()
    row_count = mapping_determinant.shape[0]
    column_count = mapping_determinant.shape[1]
    row_table = jnp.asarray(np.kron(np.eye(row_count // 4), derivative), jnp.float32)
    column_table = jnp.asarray(np.kron(np.eye(column_count // 4), derivative).T, jnp.float32)

    def along_rows(field):
        return jnp.einsum("ab,...bc->...ac", row_table, field, precision=highest)

    def along_columns(field):
        return jnp.einsum("...ab,bc->...ac", field, column_table, precision=highest)

    strip_parts_sequence = heat_state * layer_pressure_depth
    local_total = jnp.sum(strip_parts_sequence, axis=0)
    higher = carried_in(local_total, "lev", add_terms, jnp.zeros_like(local_total))
    gravity_potential_altitude = (
        ground_gravity_potential
        + higher
        + (local_total - jnp.cumsum(strip_parts_sequence, axis=0))
        + 0.5 * strip_parts_sequence
    )
    fields, courant, damping = advance(
        airflow_components[0],
        airflow_components[1],
        heat_state,
        layer_pressure_depth,
        constituent_masses,
        gravity_potential_altitude,
        inverse_mapping_entries,
        mapping_determinant,
        along_rows,
        along_columns,
    )
    courant_all, damping_all = (
        one_axis_at_a_time(courant, FACE_TILE_LEV),
        one_axis_at_a_time(damping, FACE_TILE_LEV),
    )
    stepping_bounds = jnp.stack([courant_all, damping_all])
    weight_rows = jnp.asarray(np.tile(weights, row_count // 4), jnp.float32)
    weight_columns = jnp.asarray(np.tile(weights, column_count // 4), jnp.float32)
    mass = mapping_determinant * weight_rows[:, None] * weight_columns[None, :]
    weighted = fields * mass
    mass_block = mass[None, None]
    row_padded = (extended(weighted, ((FACE, 2),), 1), extended(mass_block, ((FACE, 2),), 1))
    padded, padded_mass = (
        extended(row_padded[0], ((TILE, 3),), 1),
        extended(row_padded[1], ((TILE, 3),), 1),
    )
    face_index = lax.axis_index(FACE)
    tile_index = lax.axis_index(TILE)
    face_count = lax.axis_size(FACE)
    tile_count = lax.axis_size(TILE)
    face_lower = (face_index + face_count - 1) % face_count
    tile_lower = (tile_index + tile_count - 1) % tile_count
    rotations = (
        (4 - interface_rightangle_rotations[face_lower, tile_index, 0]) % 4,
        interface_rightangle_rotations[face_index, tile_index, 0],
        (4 - interface_rightangle_rotations[face_index, tile_lower, 1]) % 4,
        interface_rightangle_rotations[face_index, tile_index, 1],
    )
    flips = (
        interface_flipped_markers[face_lower, tile_index, 0],
        interface_flipped_markers[face_index, tile_index, 0],
        interface_flipped_markers[face_index, tile_lower, 1],
        interface_flipped_markers[face_index, tile_index, 1],
    )
    valences = (
        corner_block_tally[face_lower, tile_lower],
        corner_block_tally[face_lower, tile_index],
        corner_block_tally[face_index, tile_lower],
        corner_block_tally[face_index, tile_index],
    )
    pieces = rim_pieces(padded)
    pieces = (weighted,) + pieces[1:]
    mass_pieces = rim_pieces(padded_mass)
    mass_pieces = (mass_block,) + mass_pieces[1:]
    substep_outcome = combine_block(pieces, mass_pieces, rotations, flips, valences)
    airflow_next = substep_outcome[0:2]
    heat_state_next = substep_outcome[2]
    pressure_depth_next = substep_outcome[3]
    constituent_masses_next = substep_outcome[4:]
    return (
        airflow_next,
        heat_state_next,
        pressure_depth_next,
        constituent_masses_next,
        stepping_bounds,
    )


def solution(mesh):
    split = Mesh(
        mesh.devices.reshape(4, 4, 8, 2, mesh.shape["lev"]),
        ("face_0", "face_1", "tile_0", "tile_1", "lev"),
    )
    placed = (
        P(None, "lev", FACE, TILE),
        P("lev", FACE, TILE),
        P("lev", FACE, TILE),
        P(None, "lev", FACE, TILE),
        P(FACE, TILE),
        P(None, FACE, TILE),
        P(FACE, TILE),
        P(),
        P(),
        P(),
    )
    return jax.shard_map(
        on_device,
        mesh=split,
        in_specs=placed,
        out_specs=(
            P(None, "lev", FACE, TILE),
            P("lev", FACE, TILE),
            P("lev", FACE, TILE),
            P(None, "lev", FACE, TILE),
            P(),
        ),
        check_vma=False,
    )
```

profile of v0, /device:TPU:6, one launch (start us, length us, event | category | flops | bytes accessed | tf_op | source)
XLA Modules:
  0.0 189.9 jit_solution(15095461625676311029)
XLA Ops:
  0.7 1.0 multiply_reduce_fusion.2
  1.7 1.1 convolution_bitcast_fusion.4
  2.9 1.1 convolution_bitcast_fusion.2
  4.0 15.5 %all-gather = f32[32,128]{1,0:T(8,128)S(1)} all-gather(f32[8,128]{1,0:T(8,128)S(1)} %multiply_reduce_fusion.2), channel_id=2, replica_groups=mesh['face_0'=4,'face_1'=4,'tile_0'=8,'tile_1'=2,'lev'=4] {'lev'}, dimensions={0}, use_global_device_ids=true | all-gather | bytes 20480 | tf_op jit(solution)/shard_map/all_gather | solution.py:25
  19.6 1.1 fusion.98
  21.4 1.2 fusion.32
  25.0 1.5 convolution_bitcast_fusion
  26.5 1.4 fusion.10
  28.3 2.7 %collective-permute-start.1 = (f32[22,18,1,128]{3,2,1,0:T(1,128)S(1)}, f32[22,18,1,128]{3,2,1,0:T(1,128)S(1)}, u32[]{:S(2)}, u32[]{:S(2)}) collective-permute-start(f32[22,18,1,128]{3,2,1,0:T(1,128)S(1)} %get-tuple-element.85), channel_id=1, source_target_pairs={{64,0},{128,64},{192,128},{256,192},{320,256},{384,320},{448,384},... | collective-permute-start | bytes 608264 | tf_op jit(solution)/shard_map/ppermute | solution.py:48
  31.1 10.0 %collective-permute-start = (f32[22,18,1,128]{3,2,1,0:T(1,128)S(1)}, f32[22,18,1,128]{3,2,1,0:T(1,128)S(1)}, u32[]{:S(2)}, u32[]{:S(2)}) collective-permute-start(f32[22,18,1,128]{3,2,1,0:T(1,128)S(1)} %get-tuple-element.84), channel_id=1, source_target_pairs={{0,64},{64,128},{128,192},{192,256},{256,320},{320,384},{384,448},... | collective-permute-start | bytes 608264 | tf_op jit(solution)/shard_map/ppermute | solution.py:46
  41.1 1.9 %collective-permute-start.5 = (f32[1,1,1,128]{3,2,1,0:T(1,128)S(1)}, f32[1,1,1,128]{3,2,1,0:T(1,128)S(1)}, u32[]{:S(2)}, u32[]{:S(2)}) collective-permute-start(f32[1,1,1,128]{3,2,1,0:T(1,128)S(1)} %get-tuple-element.135), channel_id=1, source_target_pairs={{64,0},{128,64},{192,128},{256,192},{320,256},{384,320},{448,384},... | collective-permute-start | bytes 1544 | tf_op jit(solution)/shard_map/ppermute | solution.py:48
  43.0 9.9 %collective-permute-start.4 = (f32[1,1,1,128]{3,2,1,0:T(1,128)S(1)}, f32[1,1,1,128]{3,2,1,0:T(1,128)S(1)}, u32[]{:S(2)}, u32[]{:S(2)}) collective-permute-start(f32[1,1,1,128]{3,2,1,0:T(1,128)S(1)} %get-tuple-element.134), channel_id=1, source_target_pairs={{0,64},{64,128},{128,192},{192,256},{256,320},{320,384},{384,448},... | collective-permute-start | bytes 1544 | tf_op jit(solution)/shard_map/ppermute | solution.py:46
  53.0 1.5 constant_dynamic-slice_fusion.6
  63.8 1.4 fusion.96
  71.0 24.3 %all-reduce.3 = (f32[]{:T(128)}, f32[]{:T(128)}) all-reduce(f32[]{:T(128)} %get-tuple-element.138, f32[]{:T(128)} %multiply_reduce_fusion.1), channel_id=1, replica_groups=mesh['face_0'=4,'face_1'=4,'tile_0'=8,'tile_1'=2,'lev'=4] {'face_0'}, use_global_device_ids=true, to_apply=%region_11.12 | all-reduce | flops 2 | bytes 16 | tf_op jit(solution)/shard_map/pmax | solution.py:36
  95.3 8.1 %all-reduce.2 = (f32[]{:T(128)}, f32[]{:T(128)}) all-reduce(f32[]{:T(128)} %get-tuple-element.76, f32[]{:T(128)} %get-tuple-element.77), channel_id=1, replica_groups=mesh['face_0'=4,'face_1'=4,'tile_0'=8,'tile_1'=2,'lev'=4] {'face_1'}, use_global_device_ids=true, to_apply=%region_12.13 | all-reduce | flops 2 | bytes 16 | tf_op jit(solution)/shard_map/pmax | solution.py:36
  103.4 18.2 %all-reduce = (f32[]{:T(128)}, f32[]{:T(128)}) all-reduce(f32[]{:T(128)} %get-tuple-element.74, f32[]{:T(128)} %get-tuple-element.75), channel_id=1, replica_groups=mesh['face_0'=4,'face_1'=4,'tile_0'=8,'tile_1'=2,'lev'=4] {'tile_0'}, use_global_device_ids=true, to_apply=%region_13.14 | all-reduce | flops 2 | bytes 16 | tf_op jit(solution)/shard_map/pmax | solution.py:36
  121.7 3.1 %all-reduce.4 = (f32[]{:T(128)}, f32[]{:T(128)}) all-reduce(f32[]{:T(128)} %get-tuple-element.70, f32[]{:T(128)} %get-tuple-element.71), channel_id=1, replica_groups=mesh['face_0'=4,'face_1'=4,'tile_0'=8,'tile_1'=2,'lev'=4] {'tile_1'}, use_global_device_ids=true, to_apply=%region_14.15 | all-reduce | flops 2 | bytes 16 | tf_op jit(solution)/shard_map/pmax | solution.py:36
  124.7 12.3 %all-reduce.1 = (f32[1]{0:T(128)}, f32[1]{0:T(128)}) all-reduce(f32[1]{0:T(128)} %bitcast.84, f32[1]{0:T(128)} %bitcast.83), channel_id=1, replica_groups=mesh['face_0'=4,'face_1'=4,'tile_0'=8,'tile_1'=2,'lev'=4] {'lev'}, use_global_device_ids=true, to_apply=%region_15.16 | all-reduce | flops 2 | bytes 16 | tf_op jit(solution)/shard_map/pmax | solution.py:36
  137.1 1.9 pad_maximum_fusion.14
  140.7 2.7 %collective-permute-done.6 = f32[1,1,10,1]{3,2,1,0:T(8,128)S(1)} collective-permute-done((f32[1,1,10,1]{3,2,1,0:T(8,128)S(1)}, f32[1,1,10,1]{3,2,1,0:T(8,128)S(1)}, u32[]{:S(2)}, u32[]{:S(2)}) %collective-permute-start.6) | collective-permute-done | bytes 72 | tf_op jit(solution)/shard_map/ppermute | solution.py:46
  148.9 3.8 %fusion.91 = (f32[22,18,10,1]{3,2,1,0:T(8,128)}, f32[22,18,10,1]{3,2,1,0:T(8,128)}) fusion(f32[22,18,10,128]{3,2,1,0:T(8,128)S(1)} %pad_maximum_fusion.6), kind=kLoop, calls=%fused_computation.199 | loop fusion | bytes 63360 | tf_op jit(solution)/shard_map/slice | solution.py:43
  152.7 3.3 %copy.225 = f32[22,18,10,1]{0,3,2,1:T(1,128)} copy(f32[22,18,10,1]{3,2,1,0:T(8,128)} %get-tuple-element.81) | data formatting | bytes 31680 | tf_op jit(solution)/shard_map/slice | solution.py:42
  156.4 3.3 %copy.220 = f32[22,18,10,1]{0,3,2,1:T(1,128)} copy(f32[22,18,10,1]{3,2,1,0:T(8,128)} %get-tuple-element.80) | data formatting | bytes 31680 | tf_op jit(solution)/shard_map/slice | solution.py:43
  162.6 2.5 %collective-permute-done.2 = f32[22,18,10,1]{0,3,2,1:T(1,128)S(1)} collective-permute-done((f32[22,18,10,1]{0,3,2,1:T(1,128)}, f32[22,18,10,1]{0,3,2,1:T(1,128)S(1)}, u32[]{:S(2)}, u32[]{:S(2)}) %collective-permute-start.2) | collective-permute-done | bytes 15872 | tf_op jit(solution)/shard_map/ppermute | solution.py:46
  167.2 1.2 copy.247
  168.6 1.2 copy.231
  169.8 1.5 slice.319
  173.1 2.3 %copy.230 = f32[22,18,8,1]{3,2,1,0:T(8,128)} copy(f32[22,18,8,1]{1,2,0,3:T(8,128)S(1)} %maximum_bitcast_fusion.2) | data formatting | bytes 25344 | tf_op jit(solution)/shard_map/broadcast_in_dim | solution.py:162
  178.9 1.5 maximum_bitcast_fusion
  181.0 5.5 %fusion.1 = f32[22,18,8,130]{3,2,1,0:T(8,128)S(1)} fusion(f32[22,18,1,130]{3,2,1,0:T(1,128)} %copy.247, f32[22,18,8,1]{3,2,1,0:T(8,128)S(1)} %copy.231, f32[22,18,8,128]{3,2,1,0:T(8,128)S(1)} %broadcast_multiply_fusion, f32[22,18,8,1]{3,2,1,0:T(8,128)S(1)} %copy-done, f32[22,18,1,130]{3,2,1,0:T(1,128)S(1)} %copy.239, pred[8]{0:T(512)(128)(4,1)S(1)} %copy-done.19, ...), kind=kLoop, calls=%fused_computation.3 | loop fusion | flops 4942080 | bytes 3706576 | tf_op jit(solution)/shard_map/add | solution.py:172
  188.8 1.1 slice.363
  (143 shorter events, 22.1 us)
Async XLA Ops:
  0.6 22.3 %copy-start.8 = (f32[128,128,1]{1,0,2:T(8,128)S(1)}, f32[128,128,1]{1,0,2:T(8,128)}, u32[]{:S(2)}) copy-start(f32[128,128,1]{1,0,2:T(8,128)} %constant.249) | copy-start | bytes 196612
  0.6 22.0 %copy-start.7 = (f32[8,8,1]{1,0,2:T(8,128)S(1)}, f32[8,8,1]{1,0,2:T(8,128)}, u32[]{:S(2)}) copy-start(f32[8,8,1]{1,0,2:T(8,128)} %constant.248) | copy-start | bytes 772
  0.7 22.5 %copy-start.2 = (f32[18,8,128]{2,1,0:T(8,128)S(1)}, f32[18,8,128]{2,1,0:T(8,128)}, u32[]{:S(2)}) copy-start(f32[18,8,128]{2,1,0:T(8,128)} %param.18) | copy-start | bytes 221188
  0.7 22.2 %copy-start.1 = (f32[2,18,8,128]{3,2,1,0:T(8,128)S(1)}, f32[2,18,8,128]{3,2,1,0:T(8,128)}, u32[]{:S(2)}) copy-start(f32[2,18,8,128]{3,2,1,0:T(8,128)} %param.16) | copy-start | bytes 442372
  0.7 22.2 %copy-start.11 = (f32[4,8,128]{2,1,0:T(8,128)S(1)}, f32[4,8,128]{2,1,0:T(8,128)}, u32[]{:S(2)}) copy-start(f32[4,8,128]{2,1,0:T(8,128)} %param.21) | copy-start | bytes 49156
  0.7 22.4 %copy-start.9 = (f32[8,128]{1,0:T(8,128)S(1)}, f32[8,128]{1,0:T(8,128)}, u32[]{:S(2)}) copy-start(f32[8,128]{1,0:T(8,128)} %param.22) | copy-start | bytes 12292
  4.0 20.4 %copy-start.3 = (f32[18,8,128]{2,1,0:T(8,128)S(1)}, f32[18,8,128]{2,1,0:T(8,128)}, u32[]{:S(2)}) copy-start(f32[18,8,128]{2,1,0:T(8,128)} %param.17) | copy-start | bytes 221188
  19.6 5.1 %copy-start.20 = (f32[128]{0:T(128)S(1)}, f32[128]{0:T(128)}, u32[]{:S(2)}) copy-start(f32[128]{0:T(128)} %constant.240.clone) | copy-start | bytes 1540
  19.6 5.1 %copy-start.21 = (f32[8]{0:T(128)S(1)}, f32[8]{0:T(128)}, u32[]{:S(2)}) copy-start(f32[8]{0:T(128)} %constant.239.clone) | copy-start | bytes 100
  21.4 3.6 %copy-start.22 = (f32[18,18,8,128]{3,2,1,0:T(8,128)S(1)}, f32[18,18,8,128]{3,2,1,0:T(8,128)}, u32[]{:S(2)}) copy-start(f32[18,18,8,128]{3,2,1,0:T(8,128)} %param.19) | copy-start | bytes 3981316
  21.4 3.6 %copy-start.24 = (f32[8,8,1,1]{1,0,3,2:T(8,128)S(1)}, f32[8,8,1,1]{1,0,3,2:T(8,128)}, u32[]{:S(2)}) copy-start(f32[8,8,1,1]{1,0,3,2:T(8,128)} %constant.250) | copy-start | bytes 772
  25.0 1.5 copy-start.23
  28.3 119.9 %collective-permute-start.1 = (f32[22,18,1,128]{3,2,1,0:T(1,128)S(1)}, f32[22,18,1,128]{3,2,1,0:T(1,128)S(1)}, u32[]{:S(2)}, u32[]{:S(2)}) collective-permute-start(f32[22,18,1,128]{3,2,1,0:T(1,128)S(1)} %get-tuple-element.85), channel_id=1, source_target_pairs={{64,0},{128,64},{192,128},{256,192},{320,256},{384,320},{448,384},... | collective-permute-start | bytes 608264 | tf_op jit(solution)/shard_map/ppermute | solution.py:48
  31.1 117.1 %collective-permute-start = (f32[22,18,1,128]{3,2,1,0:T(1,128)S(1)}, f32[22,18,1,128]{3,2,1,0:T(1,128)S(1)}, u32[]{:S(2)}, u32[]{:S(2)}) collective-permute-start(f32[22,18,1,128]{3,2,1,0:T(1,128)S(1)} %get-tuple-element.84), channel_id=1, source_target_pairs={{0,64},{64,128},{128,192},{192,256},{256,320},{320,384},{384,448},... | collective-permute-start | bytes 608264 | tf_op jit(solution)/shard_map/ppermute | solution.py:46
  41.1 97.9 %collective-permute-start.5 = (f32[1,1,1,128]{3,2,1,0:T(1,128)S(1)}, f32[1,1,1,128]{3,2,1,0:T(1,128)S(1)}, u32[]{:S(2)}, u32[]{:S(2)}) collective-permute-start(f32[1,1,1,128]{3,2,1,0:T(1,128)S(1)} %get-tuple-element.135), channel_id=1, source_target_pairs={{64,0},{128,64},{192,128},{256,192},{320,256},{384,320},{448,384},... | collective-permute-start | bytes 1544 | tf_op jit(solution)/shard_map/ppermute | solution.py:48
  43.0 95.9 %collective-permute-start.4 = (f32[1,1,1,128]{3,2,1,0:T(1,128)S(1)}, f32[1,1,1,128]{3,2,1,0:T(1,128)S(1)}, u32[]{:S(2)}, u32[]{:S(2)}) collective-permute-start(f32[1,1,1,128]{3,2,1,0:T(1,128)S(1)} %get-tuple-element.134), channel_id=1, source_target_pairs={{0,64},{64,128},{128,192},{192,256},{256,320},{320,384},{384,448},... | collective-permute-start | bytes 1544 | tf_op jit(solution)/shard_map/ppermute | solution.py:46
  63.7 85.1 %copy-start.16 = (pred[8]{0:T(512)(128)(4,1)}, pred[8]{0:T(512)(128)(4,1)S(1)}, u32[]{:S(2)}) copy-start(pred[8]{0:T(512)(128)(4,1)S(1)} %get-tuple-element.142) | copy-start | bytes 28
  63.7 85.1 %copy-start.18 = (pred[8]{0:T(512)(128)(4,1)}, pred[8]{0:T(512)(128)(4,1)S(1)}, u32[]{:S(2)}) copy-start(pred[8]{0:T(512)(128)(4,1)S(1)} %get-tuple-element.143) | copy-start | bytes 28
  63.7 85.1 %copy-start.12 = (pred[128]{0:T(512)(128)(4,1)}, pred[128]{0:T(512)(128)(4,1)S(1)}, u32[]{:S(2)}) copy-start(pred[128]{0:T(512)(128)(4,1)S(1)} %get-tuple-element.140) | copy-start | bytes 388
  63.7 85.1 %copy-start.14 = (pred[128]{0:T(512)(128)(4,1)}, pred[128]{0:T(512)(128)(4,1)S(1)}, u32[]{:S(2)}) copy-start(pred[128]{0:T(512)(128)(4,1)S(1)} %get-tuple-element.141) | copy-start | bytes 388
  139.0 1.4 collective-permute-start.7
  139.1 4.3 %collective-permute-start.6 = (f32[1,1,10,1]{3,2,1,0:T(8,128)S(1)}, f32[1,1,10,1]{3,2,1,0:T(8,128)S(1)}, u32[]{:S(2)}, u32[]{:S(2)}) collective-permute-start(f32[1,1,10,1]{3,2,1,0:T(8,128)S(1)} %get-tuple-element.126), channel_id=1, source_target_pairs={{0,4},{4,8},{8,12},{12,16},{16,20},{20,24},{24,28},{28,32},{32,36}... | collective-permute-start | bytes 128 | tf_op jit(solution)/shard_map/ppermute | solution.py:46
  156.0 4.9 %collective-permute-start.3 = (f32[22,18,10,1]{0,3,2,1:T(1,128)}, f32[22,18,10,1]{0,3,2,1:T(1,128)S(1)}, u32[]{:S(2)}, u32[]{:S(2)}) collective-permute-start(f32[22,18,10,1]{0,3,2,1:T(1,128)} %copy.225), channel_id=1, source_target_pairs={{4,0},{8,4},{12,8},{16,12},{20,16},{24,20},{28,24},{32,28},{36,32}... | collective-permute-start | bytes 47528 | tf_op jit(solution)/shard_map/ppermute | solution.py:48
  159.7 5.4 %collective-permute-start.2 = (f32[22,18,10,1]{0,3,2,1:T(1,128)}, f32[22,18,10,1]{0,3,2,1:T(1,128)S(1)}, u32[]{:S(2)}, u32[]{:S(2)}) collective-permute-start(f32[22,18,10,1]{0,3,2,1:T(1,128)} %copy.220), channel_id=1, source_target_pairs={{0,4},{4,8},{8,12},{12,16},{16,20},{20,24},{24,28},{28,32},{32,36}... | collective-permute-start | bytes 47528 | tf_op jit(solution)/shard_map/ppermute | solution.py:46
  162.4 6.0 %copy-start.6 = (f32[22,18,10,1]{0,3,2,1:T(1,128)S(1)}, f32[22,18,10,1]{0,3,2,1:T(1,128)}, u32[]{:S(2)}) copy-start(f32[22,18,10,1]{0,3,2,1:T(1,128)} %copy-done.5) | copy-start | bytes 47524
  165.1 3.5 %copy-start.4 = (f32[22,18,10,1]{0,3,2,1:T(1,128)}, f32[22,18,10,1]{0,3,2,1:T(1,128)S(1)}, u32[]{:S(2)}) copy-start(f32[22,18,10,1]{0,3,2,1:T(1,128)S(1)} %collective-permute-done.2) | copy-start | bytes 47524
  175.4 5.5 %copy-start.17 = (pred[8]{0:T(512)(128)(4,1)S(1)}, pred[8]{0:T(512)(128)(4,1)}, u32[]{:S(2)}) copy-start(pred[8]{0:T(512)(128)(4,1)} %copy-done.16) | copy-start | bytes 28
  175.4 5.5 %copy-start.19 = (pred[8]{0:T(512)(128)(4,1)S(1)}, pred[8]{0:T(512)(128)(4,1)}, u32[]{:S(2)}) copy-start(pred[8]{0:T(512)(128)(4,1)} %copy-done.18) | copy-start | bytes 28
  178.9 2.0 %copy-start = (f32[22,18,8,1]{3,2,1,0:T(8,128)S(1)}, f32[22,18,8,1]{3,2,1,0:T(8,128)}, u32[]{:S(2)}) copy-start(f32[22,18,8,1]{3,2,1,0:T(8,128)} %copy.230) | copy-start | bytes 38020
  180.9 5.6 %copy-start.10 = (f32[8,128]{1,0:T(8,128)S(1)}, f32[8,128]{1,0:T(8,128)}, u32[]{:S(2)}) copy-start(f32[8,128]{1,0:T(8,128)} %fusion.86) | copy-start | bytes 12292
  181.0 5.6 %copy-start.13 = (pred[128]{0:T(512)(128)(4,1)S(1)}, pred[128]{0:T(512)(128)(4,1)}, u32[]{:S(2)}) copy-start(pred[128]{0:T(512)(128)(4,1)} %copy-done.12) | copy-start | bytes 388
  181.0 5.6 %copy-start.15 = (pred[128]{0:T(512)(128)(4,1)S(1)}, pred[128]{0:T(512)(128)(4,1)}, u32[]{:S(2)}) copy-start(pred[128]{0:T(512)(128)(4,1)} %copy-done.14) | copy-start | bytes 388
  (1 other events, 1.4 us)
where the time goes:
time: 193 us; the launch traced here: 190 us
  blocking collectives  81.6 us (42%)
  local copies, waits for them, and re-layouts  30.6 us (16%)
  starting transfers between devices  25.6 us (13%)
  other arithmetic  19.6 us (10%)
  between operations  18.3 us (9%)
  matrix products  8.36 us (4%)
  waiting for transfers between devices  5.87 us (3%)
    pmax x5, blocking collectives, one_axis_at_a_time(): return functools.reduce(lax.pmax, axes, x)  66.1 us
    ppermute x4, starting transfers between devices, extended(): lax.ppermute(tail, axis, [(i, (i + 1) % count) for i in range(count)])  20.8 us
    all_gather x1, blocking collectives, carried_in(): gathered = lax.all_gather(part, axis)  15.5 us
    slice x5, local copies, waits for them, and re-layouts, extended(): lax.slice_in_dim(cells, cells.shape[dim] - width, cells.shape[dim], axis=...  7.47 us
    add x2, other arithmetic, shared_sums(): padded[..., 1:-1, :] + jnp.where(row_low, padded[..., :-2, :], 0.0)  5.6 us
    ppermute x4, waiting for transfers between devices, extended(): lax.ppermute(tail, axis, [(i, (i + 1) % count) for i in range(count)])  5.2 us
    dot_general x6, matrix products, along_columns(): return jnp.einsum('...ab,bc->...ac', field, column_table, precision=highest)  4.93 us
    ppermute x4, starting transfers between devices, extended(): lax.ppermute(head, axis, [((i + 1) % count, i) for i in range(count)])  4.88 us
  transfers between devices with their start and end apart: 8, of which 3 were waited for; matrix products, arithmetic and copies ran while one was open for 8% of the time, Pallas kernels for 0%

commit v1 on v0

v1 whole, which is shorter than its diff:
```python
import math

import jax
import jax.numpy as jnp
import numpy as np
from jax import lax
from jax.experimental import pallas as pl
from jax.experimental.pallas import tpu as pltpu
from jax.sharding import Mesh
from jax.sharding import PartitionSpec as P

FACE = ("face_0", "face_1")
TILE = ("tile_0", "tile_1")
PLANE = ("face_1", "tile_0", "tile_1")

time_step = 0.05
viscosity = 0.05

PER_GROUP = 6
ROWS, LANES = 8, 128
VMEM = pl.BlockSpec(memory_space=pltpu.VMEM)
SMEM = pl.BlockSpec(memory_space=pltpu.SMEM)


def gll_tables():
    offset = 1.0 / math.sqrt(5.0)
    nodes = np.array([-1.0, -offset, offset, 1.0])
    weights = np.array([1.0 / 6.0, 5.0 / 6.0, 5.0 / 6.0, 1.0 / 6.0])
    bary = np.ones(4)
    for i in range(4):
        for j in range(4):
            if j != i:
                bary[i] = bary[i] / (nodes[i] - nodes[j])
    derivative = np.zeros((4, 4))
    for i in range(4):
        for j in range(4):
            if j != i:
                derivative[i, j] = bary[j] / bary[i] / (nodes[i] - nodes[j])
        derivative[i, i] = -np.sum(derivative[i])
    return derivative, weights


DERIVATIVE, WEIGHTS = gll_tables()


def iota(axis):
    return lax.broadcasted_iota(jnp.int32, (ROWS, LANES), axis)


def by_node(place, values):
    node = place % 4
    plane = jnp.full((ROWS, LANES), float(values[0]), jnp.float32)
    for i in range(1, 4):
        plane = jnp.where(node == i, float(values[i]), plane)
    return plane


def node_weights():
    return by_node(iota(0), WEIGHTS) * by_node(iota(1), WEIGHTS)


def derivative_terms(axis, scale):
    place = iota(axis)
    terms = []
    for k in range(-3, 4):
        values = [DERIVATIVE[i, i + k] if 0 <= i + k < 4 else 0.0 for i in range(4)]
        terms.append((k, by_node(place, values) * scale))
    return terms


def derive(field, axis, terms):
    size = field.shape[axis]
    total = None
    for k, coefficient in terms:
        moved = field if k == 0 else pltpu.roll(field, (-k) % size, axis)
        part = coefficient * moved
        total = part if total is None else total + part
    return total


def tile_of(index):
    return pl.ds(pl.multiple_of(index * ROWS, ROWS), ROWS)


def local_kernel(n_lev, air, heat, thick, tracer, ground, maps, det, w_out, left_out, right_out, share_out):
    levels = heat.shape[0]
    tracers = tracer.shape[0]
    fields = 4 + tracers
    groups = left_out.shape[0]
    lane = iota(1)
    ww = node_weights()
    j = det[...]
    mass = j * ww
    m00, m01, m10, m11 = maps[0], maps[1], maps[2], maps[3]
    j00, j01, j10, j11 = j * m00, j * m01, j * m10, j * m11
    scale = time_step * ww
    undo = 1.0 / scale
    b11 = (j00 * m00 + j01 * m01) * undo
    b12 = (j00 * m10 + j01 * m11) * undo
    b22 = (j10 * m10 + j11 * m11) * undo
    along_rows = derivative_terms(0, scale)
    along_columns = derivative_terms(1, scale)
    ground_plane = ground[...]

    def flux(first, second):
        return derive(first, 0, along_rows) + derive(second, 1, along_columns)

    def one(turn, carry):
        below, speed, damp, lefts, rights = carry
        lefts, rights = list(lefts), list(rights)
        level = levels - 1 - turn
        u, v = air[0, level], air[1, level]
        heat_l, thick_l = heat[level], thick[level]
        relative = lane - level

        def put(field, value):
            w_out[tile_of(field * levels + level), :] = value
            group = field // PER_GROUP
            here = relative == (field % PER_GROUP) * levels
            lefts[group] = jnp.where(here, value[:, 0:1], lefts[group])
            rights[group] = jnp.where(here, value[:, LANES - 1 : LANES], rights[group])

        term = heat_l * thick_l
        square = u * u + v * v
        energy = 0.5 * square + (ground_plane + below + 0.5 * term)
        below = below + term
        speed = jnp.maximum(speed, square)
        first, second = j00 * u + j01 * v, j10 * u + j11 * v

        rows, columns = derive(energy, 0, along_rows), derive(energy, 1, along_columns)
        put(0, mass * u - (j00 * rows + j10 * columns))
        put(1, mass * v - (j01 * rows + j11 * columns))
        rows, columns = derive(heat_l, 0, along_rows), derive(heat_l, 1, along_columns)
        put(2, mass * heat_l - (first * rows + second * columns))
        rows, columns = derive(thick_l, 0, along_rows), derive(thick_l, 1, along_columns)
        laplace = flux(b11 * rows + b12 * columns, b12 * rows + b22 * columns)
        damp = jnp.maximum(damp, jnp.abs(laplace))
        put(3, mass * thick_l - flux(thick_l * first, thick_l * second) + viscosity * laplace)
        for t in range(tracers):
            q = tracer[t, level]
            put(4 + t, mass * q - flux(q * first, q * second))
        return below, speed, damp, tuple(lefts), tuple(rights)

    zero = jnp.zeros((ROWS, LANES), jnp.float32)
    none = tuple(zero for _ in range(groups))
    total, speed, damp, lefts, rights = lax.fori_loop(0, levels, one, (zero, zero, zero, none, none))
    group, here = fields // PER_GROUP, lane == (fields % PER_GROUP) * levels
    lefts, rights = list(lefts), list(rights)
    lefts[group] = jnp.where(here, mass[:, 0:1], lefts[group])
    rights[group] = jnp.where(here, mass[:, LANES - 1 : LANES], rights[group])
    for g in range(groups):
        left_out[g] = lefts[g]
        right_out[g] = rights[g]
    w_out[pl.ds(fields * levels * ROWS, ROWS), :] = mass
    spare = w_out.shape[0] - (fields * levels + 1) * ROWS
    w_out[pl.ds((fields * levels + 1) * ROWS, spare), :] = jnp.zeros((spare, LANES), jnp.float32)
    spacing = jnp.sqrt(m00 * m00 + m01 * m01 + m10 * m10 + m11 * m11)
    courant = jnp.max(time_step * jnp.sqrt(speed) * spacing, axis=0, keepdims=True)
    damping = jnp.max(damp * (viscosity / mass), axis=0, keepdims=True)
    row = iota(0)
    bounds = jnp.where(row == 0, courant, damping)
    for peer in range(n_lev):
        share_out[peer, pl.ds(0, ROWS), :] = total
        share_out[peer, pl.ds(ROWS, ROWS), :] = bounds


def carry_kernel(levels, shared, w, lefts, rights, maps, det, wind_out, top_out, bottom_out, left_out, right_out, bound_out):
    me = lax.axis_index("lev")
    higher = jnp.zeros((ROWS, LANES), jnp.float32)
    bounds = shared[0, pl.ds(ROWS, ROWS), :]
    for peer in range(shared.shape[0]):
        higher = higher + jnp.where(peer > me, shared[peer, pl.ds(0, ROWS), :], 0.0)
        bounds = jnp.maximum(bounds, shared[peer, pl.ds(ROWS, ROWS), :])
    lane = iota(1)
    both = jnp.maximum(bounds, pltpu.roll(bounds, LANES // 2, 1))
    line = jnp.where(lane[0:1] < LANES // 2, both[0:1], both[1:2])
    bound_out[...] = jnp.broadcast_to(line[None], bound_out.shape)

    ww = node_weights()
    j = det[...]
    rows = derive(higher, 0, derivative_terms(0, time_step * ww))
    columns = derive(higher, 1, derivative_terms(1, time_step * ww))
    add_u = -j * (maps[0] * rows + maps[2] * columns)
    add_v = -j * (maps[1] * rows + maps[3] * columns)
    for field, add in ((0, add_u), (1, add_v)):
        for level in range(levels):
            at = pl.ds((field * levels + level) * ROWS, ROWS)
            wind_out[at, :] = w[at, :] + add
    is_u, is_v = lane < levels, (lane >= levels) & (lane < 2 * levels)

    def with_higher(ref, group, at):
        value = ref[group]
        if group == 0:
            value = value + jnp.where(is_u, add_u[:, at : at + 1], jnp.where(is_v, add_v[:, at : at + 1], 0.0))
        return value

    groups = lefts.shape[0]
    edge_rows = top_out.shape[0] - 2 * groups
    winds = 2 * levels
    for source, out, row in ((w, top_out, ROWS - 1), (w, bottom_out, 0)):
        for start in range(0, edge_rows, ROWS):
            out[pl.ds(start, ROWS), :] = source[pl.ds(start * ROWS + row, ROWS, stride=ROWS), :]
        out[pl.ds(0, levels), :] = out[pl.ds(0, levels), :] + add_u[row : row + 1]
        out[pl.ds(levels, levels), :] = out[pl.ds(levels, levels), :] + add_v[row : row + 1]
    for g in range(groups):
        left, right = with_higher(lefts, g, 0), with_higher(rights, g, LANES - 1)
        left_out[pl.ds(g * ROWS, ROWS), :] = left
        right_out[pl.ds(g * ROWS, ROWS), :] = right
        for out, row in ((top_out, ROWS - 1), (bottom_out, 0)):
            out[pl.ds(edge_rows + g, 1), :] = left[row : row + 1]
            out[pl.ds(edge_rows + groups + g, 1), :] = right[row : row + 1]


def turned(u, v, code):
    cosine = jnp.where(code == 0, 1.0, jnp.where(code == 2, -1.0, 0.0)).astype(jnp.float32)
    sine = jnp.where(code == 1, 1.0, jnp.where(code == 3, -1.0, 0.0)).astype(jnp.float32)
    return cosine * u - sine * v, sine * u + cosine * v


def sum_kernel(
    levels, n_face, n_tile, rotations, flips, valences, w, wind, up, down, west, east,
    air_out, heat_out, thick_out, tracer_out, up_rim, down_rim, west_rim, east_rim,
):
    face, tile = lax.axis_index(FACE), lax.axis_index(TILE)
    face_lower = lax.rem(face + n_face - 1, n_face)
    tile_lower = lax.rem(tile + n_tile - 1, n_tile)

    def at(f, t):
        return f * n_tile + t

    top_code = (4 - rotations[2 * at(face_lower, tile)]) & 3
    bottom_code = rotations[2 * at(face, tile)]
    west_code = (4 - rotations[2 * at(face, tile_lower) + 1]) & 3
    east_code = rotations[2 * at(face, tile) + 1]
    top_flip = flips[2 * at(face_lower, tile)]
    bottom_flip = flips[2 * at(face, tile)]
    west_flip = flips[2 * at(face, tile_lower) + 1]
    east_flip = flips[2 * at(face, tile) + 1]
    corners = {
        ("up", "west"): valences[at(face_lower, tile_lower)],
        ("up", "east"): valences[at(face_lower, tile)],
        ("down", "west"): valences[at(face, tile_lower)],
        ("down", "east"): valences[at(face, tile)],
    }
    row, lane = iota(0), iota(1)
    tracers = tracer_out.shape[0]
    fields = 4 + tracers
    groups = west_rim.shape[0]

    edge_rows = up_rim.shape[0]
    for source, out, flag in ((up, up_rim, top_flip), (down, down_rim, bottom_flip)):
        places = jnp.where(flag == 1, LANES - 1 - lane, lane)
        for start in range(0, edge_rows, ROWS):
            rows = pl.ds(start, ROWS)
            out[rows, :] = jnp.take_along_axis(source[rows, :], places, axis=1, mode="promise_in_bounds")

    def turn_packed(x, code):
        cosine = jnp.where(code == 0, 1.0, jnp.where(code == 2, -1.0, 0.0)).astype(jnp.float32)
        sine = jnp.where(code == 1, 1.0, jnp.where(code == 3, -1.0, 0.0)).astype(jnp.float32)
        later, earlier = pltpu.roll(x, LANES - levels, 1), pltpu.roll(x, levels, 1)
        out = cosine * x + sine * jnp.where(lane < levels, -later, earlier)
        return jnp.where(lane < 2 * levels, out, x)

    for source, out, flag, code, side in (
        (west, west_rim, west_flip, west_code, "west"),
        (east, east_rim, east_flip, east_code, "east"),
    ):
        for g in range(groups):
            x = source[pl.ds(g * ROWS, ROWS), :]
            backwards = jnp.concatenate(
                [source[pl.ds(g * ROWS + ROWS - 1 - r, 1), :] for r in range(ROWS)], axis=0
            )
            x = jnp.where(flag == 1, backwards, x)
            ends = []
            for end, row_code, start in (
                ("up", top_code, groups * ROWS),
                ("down", bottom_code, groups * ROWS + groups),
            ):
                corner = jnp.broadcast_to(source[pl.ds(start + g, 1), :], (ROWS, LANES))
                if g == 0:
                    corner = turn_packed(corner, (row_code + code) & 3)
                ends.append(jnp.where(corners[end, side] == 4, corner, 0.0))
            if g == 0:
                x = turn_packed(x, code)
            beside = jnp.where(row == 3, pltpu.roll(x, ROWS - 1, 0), jnp.where(row == 4, pltpu.roll(x, 1, 0), 0.0))
            beside = jnp.where(row == 0, ends[0], jnp.where(row == ROWS - 1, ends[1], beside))
            out[g] = x + beside

    first, last = lane == 0, lane == LANES - 1
    starts, stops = lane % 4 == 0, lane % 4 == 3

    def summed(x, upper, lower, west_column, east_column):
        beside = jnp.where(row == 3, pltpu.roll(x, ROWS - 1, 0), jnp.where(row == 4, pltpu.roll(x, 1, 0), 0.0))
        beside = jnp.where(row == 0, upper, jnp.where(row == ROWS - 1, lower, beside))
        x = x + beside
        beside = jnp.where(stops, pltpu.roll(x, LANES - 1, 1), jnp.where(starts, pltpu.roll(x, 1, 1), 0.0))
        beside = jnp.where(first, west_column, jnp.where(last, east_column, beside))
        return x + beside

    def rim(ref, index):
        return jnp.broadcast_to(ref[pl.ds(index, 1), :], (ROWS, LANES))

    def columns(packed, slot, place):
        return pltpu.roll(packed, (place - slot) % LANES, 1)

    index = fields * levels
    group, slot = fields // PER_GROUP, (fields % PER_GROUP) * levels
    mass = summed(
        w[pl.ds(index * ROWS, ROWS), :], rim(up_rim, index), rim(down_rim, index),
        columns(west_rim[group], slot, 0), columns(east_rim[group], slot, LANES - 1),
    )
    scale = 1.0 / mass

    def one(level, _):
        shift = lax.rem(LANES - level, LANES)
        wests = [pltpu.roll(west_rim[g], shift, 1) for g in range(groups)]
        easts = [pltpu.roll(east_rim[g], shift, 1) for g in range(groups)]

        def out(field, x, upper, lower):
            group, slot = field // PER_GROUP, (field % PER_GROUP) * levels
            sums = summed(x, upper, lower, columns(wests[group], slot, 0), columns(easts[group], slot, LANES - 1))
            return sums * scale

        u_at, v_at = level, levels + level
        upper = turned(rim(up_rim, u_at), rim(up_rim, v_at), top_code)
        lower = turned(rim(down_rim, u_at), rim(down_rim, v_at), bottom_code)
        air_out[0, level] = out(0, wind[tile_of(u_at), :], upper[0], lower[0])
        air_out[1, level] = out(1, wind[tile_of(v_at), :], upper[1], lower[1])

        def plain(field):
            index = field * levels + level
            return out(field, w[tile_of(index), :], rim(up_rim, index), rim(down_rim, index))

        heat_out[level] = plain(2)
        thick_out[level] = plain(3)
        for t in range(tracers):
            tracer_out[t, level] = plain(4 + t)
        return 0

    lax.fori_loop(0, levels, one, 0)


def shift(x, axes, step):
    count = lax.axis_size(axes)
    return lax.ppermute(x, axes, [(i, (i + step) % count) for i in range(count)])


def on_device(air, heat, thick, tracer, ground, maps, det, rotations, flips, valences):
    levels = heat.shape[0]
    tracers = tracer.shape[0]
    fields = 4 + tracers
    tiles = fields * levels + 1
    edge_rows = -(-tiles // ROWS) * ROWS
    groups = fields // PER_GROUP + 1
    n_lev = lax.axis_size("lev")
    n_face, n_tile = lax.axis_size(FACE), lax.axis_size(TILE)
    n_plane = lax.axis_size(PLANE)

    def f32(*shape):
        return jax.ShapeDtypeStruct(shape, jnp.float32)

    params = pltpu.CompilerParams(vmem_limit_bytes=24 * 1024 * 1024)
    w, lefts, rights, share = pl.pallas_call(
        lambda *refs: local_kernel(n_lev, *refs),
        out_shape=(f32(edge_rows * ROWS, LANES), f32(groups, ROWS, LANES), f32(groups, ROWS, LANES), f32(n_lev, 2 * ROWS, LANES)),
        in_specs=[VMEM] * 7,
        out_specs=(VMEM,) * 4,
        compiler_params=params,
        name="local",
    )(air, heat, thick, tracer, ground, maps, det)
    shared = lax.all_to_all(share, "lev", 0, 0, tiled=True)
    wind, top, bottom, left, right, bound = pl.pallas_call(
        lambda *refs: carry_kernel(levels, *refs),
        out_shape=(
            f32(2 * levels * ROWS, LANES),
            f32(edge_rows + 2 * groups, LANES),
            f32(edge_rows + 2 * groups, LANES),
            f32(groups * ROWS, LANES),
            f32(groups * ROWS, LANES),
            f32(n_plane, 1, LANES),
        ),
        in_specs=[VMEM] * 6,
        out_specs=(VMEM,) * 6,
        compiler_params=params,
        name="carry",
    )(shared, w, lefts, rights, maps, det)
    up = shift(top, FACE, 1)
    down = shift(bottom, FACE, -1)
    plane = lax.all_to_all(bound, PLANE, 0, 0, tiled=True)
    bounds = lax.pmax(jnp.max(plane[:, 0, :], axis=0), "face_0")
    stepping_bounds = jnp.max(bounds.reshape(2, LANES // 2), axis=1)
    ends = edge_rows + groups
    to_east = jnp.concatenate([right, up[ends:], down[ends:]], 0)
    to_west = jnp.concatenate([left, up[edge_rows:ends], down[edge_rows:ends]], 0)
    west = shift(to_east, TILE, 1)
    east = shift(to_west, TILE, -1)
    air_next, heat_next, thick_next, tracer_next = pl.pallas_call(
        lambda *refs: sum_kernel(levels, n_face, n_tile, *refs),
        out_shape=(f32(*air.shape), f32(*heat.shape), f32(*thick.shape), f32(*tracer.shape)),
        in_specs=[SMEM] * 3 + [VMEM] * 6,
        out_specs=(VMEM,) * 4,
        scratch_shapes=[
            pltpu.VMEM((edge_rows, LANES), jnp.float32),
            pltpu.VMEM((edge_rows, LANES), jnp.float32),
            pltpu.VMEM((groups, ROWS, LANES), jnp.float32),
            pltpu.VMEM((groups, ROWS, LANES), jnp.float32),
        ],
        compiler_params=params,
        name="sum",
    )(rotations.reshape(-1), flips.reshape(-1), valences.reshape(-1), w, wind, up, down, west, east)
    return air_next, heat_next, thick_next, tracer_next, stepping_bounds


def solution(mesh):
    face, tile, lev = mesh.shape["face"], mesh.shape["tile"], mesh.shape["lev"]
    inner = min(face, 4)
    split = Mesh(
        mesh.devices.reshape(face // inner, inner, tile // 2, 2, lev),
        ("face_0", "face_1", "tile_0", "tile_1", "lev"),
    )
    level_plane = P("lev", FACE, TILE)
    field_level_plane = P(None, "lev", FACE, TILE)
    return jax.shard_map(
        on_device,
        mesh=split,
        in_specs=(
            field_level_plane, level_plane, level_plane, field_level_plane,
            P(FACE, TILE), P(None, FACE, TILE), P(FACE, TILE), P(), P(), P(),
        ),
        out_specs=(field_level_plane, level_plane, level_plane, field_level_plane, P()),
        check_vma=False,
    )
```

time: 193 us -> 112 us (0.58); the launches traced: 190 us -> 111 us
  blocking collectives: 81.6 us -> 29.5 us
  local copies, waits for them, and re-layouts: 30.6 us -> 6.88 us
  waiting for transfers between devices: 5.87 us -> 26.1 us
  Pallas kernels: 0 us -> 20.1 us
  other arithmetic: 19.6 us -> 0.73 us
  between operations: 18.3 us -> 0.73 us
  matrix products: 8.36 us -> 0 us
    pmax x5 -> x1, blocking collectives: 66.1 us -> 16.6 us  [on_device(): bounds = lax.pmax(jnp.max(plane[:, 0, :], axis=0), 'face_0')]
    ppermute x8 -> x4, waiting for transfers between devices: 5.87 us -> 26.1 us  [shift(): lax.ppermute(x, axes, [(i, (i + step) % count) for i in range(count)])]
    pallas_call x0 -> x3, Pallas kernels: none -> 20.1 us  [the longest x1 13.8 us: on_device(): pl.pallas_call(lambda *refs: local_kernel(n_lev, *refs), out_shape=(f32(e...]
    all_gather x1 -> x0, blocking collectives: 15.5 us -> none  [carried_in(): gathered = lax.all_gather(part, axis)]
    slice x18 -> x2, local copies, waits for them, and re-layouts: 15.5 us -> 0.01 us  [the longest x1 0.01 us: on_device(): up[edge_rows:ends]]
    all_to_all x0 -> x1, blocking collectives: none -> 12.8 us  [on_device(): shared = lax.all_to_all(share, 'lev', 0, 0, tiled=True)]
    all_to_all x0 -> x1, starting transfers between devices: none -> 10.5 us  [on_device(): plane = lax.all_to_all(bound, PLANE, 0, 0, tiled=True)]
    ppermute x8 -> x4, starting transfers between devices: 25.6 us -> 16.4 us  [shift(): lax.ppermute(x, axes, [(i, (i + step) % count) for i in range(count)])]
  transfers between devices with their start and end apart: 8 -> 5, of which waited for: 3 -> 1; matrix products, arithmetic and copies ran while one was open for 8% -> 1% of each run, Pallas kernels for 0% -> 0%
where the time goes in v1:
time: 112 us; the launch traced here: 111 us
  blocking collectives  29.5 us (26%)
  starting transfers between devices  27 us (24%)
  waiting for transfers between devices  26.1 us (23%)
  Pallas kernels  20.1 us (18%)
  local copies, waits for them, and re-layouts  6.88 us (6%)
    ppermute x4, waiting for transfers between devices, shift(): lax.ppermute(x, axes, [(i, (i + step) % count) for i in range(count)])  26.1 us
    pmax x1, blocking collectives, on_device(): bounds = lax.pmax(jnp.max(plane[:, 0, :], axis=0), 'face_0')  16.6 us
    ppermute x4, starting transfers between devices, shift(): lax.ppermute(x, axes, [(i, (i + step) % count) for i in range(count)])  16.4 us
    pallas_call x1, Pallas kernels, on_device(): pl.pallas_call(lambda *refs: local_kernel(n_lev, *refs), out_shape=(f32(e...  13.8 us
    all_to_all x1, blocking collectives, on_device(): shared = lax.all_to_all(share, 'lev', 0, 0, tiled=True)  12.8 us
    all_to_all x1, starting transfers between devices, on_device(): plane = lax.all_to_all(bound, PLANE, 0, 0, tiled=True)  10.5 us
    unnamed x22, local copies, waits for them, and re-layouts  6.43 us
    pallas_call x1, Pallas kernels, on_device(): pl.pallas_call(lambda *refs: sum_kernel(levels, n_face, n_tile, *refs), o...  5.48 us
  transfers between devices with their start and end apart: 5, of which 1 were waited for; matrix products, arithmetic and copies ran while one was open for 1% of the time, Pallas kernels for 0%

profile of v1, /device:TPU:6, one launch (start us, length us, event | category | flops | bytes accessed | tf_op | source)
XLA Modules:
  0.0 111.0 jit_solution(5288708326515994699)
XLA Ops:
  0.6 0.0 copy-start
  0.6 1.3 %copy-done = f32[18,18,8,128]{3,2,1,0:T(8,128)S(1)} copy-done((f32[18,18,8,128]{3,2,1,0:T(8,128)S(1)}, f32[18,18,8,128]{3,2,1,0:T(8,128)}, u32[]{:S(2)}) %copy-start) | copy-done | bytes 1327128
  2.0 0.9 copy-done.1
  2.9 0.9 copy-done.2
  3.8 0.9 copy-done.3
  4.6 0.7 copy-done.4
  5.4 0.7 copy-done.5
  6.0 0.7 copy-done.6
  6.7 13.8 %local.1 = (f32[3200,128]{1,0:T(8,128)S(1)}, f32[4,8,128]{2,1,0:T(8,128)S(1)}, f32[4,8,128]{2,1,0:T(8,128)S(1)}, f32[4,16,128]{2,1,0:T(8,128)S(1)}) custom-call(f32[2,18,8,128]{3,2,1,0:T(8,128)S(1)} %copy-done.1, f32[18,8,128]{2,1,0:T(8,128)S(1)} %copy-done.2, f32[18,8,128]{2,1,0:T(8,128)S(1)} %copy-done.3, f32[18,18,8,128]{3,2,1,0:T(8,128)S(1)} %copy-done, ...), custom_call_target="tpu_custom_call" | custom-call | tf_op jit(solution)/shard_map/local/pallas_call | solution.py:363
  20.5 12.8 %all_to_all.10.refs_0_ = f32[4,16,128]{2,1,0:T(8,128)S(1)} all-to-all(f32[4,16,128]{2,1,0:T(8,128)S(1)} %get-tuple-element.20), channel_id=1, replica_groups=mesh['face_0'=4,'face_1'=4,'tile_0'=8,'tile_1'=2,'lev'=4] {'lev'}, dimensions={0} | all-to-all | bytes 65536 | tf_op jit(solution)/shard_map/all_to_all | solution.py:371
  33.4 0.8 carry.1
  34.2 10.8 %collective-permute-start = (f32[408,128]{1,0:T(8,128)S(1)}, f32[408,128]{1,0:T(8,128)S(1)}, u32[]{:S(2)}, u32[]{:S(2)}) collective-permute-start(f32[408,128]{1,0:T(8,128)S(1)} %get-tuple-element.24), channel_id=1, source_target_pairs={{0,64},{64,128},{128,192},{192,256},{256,320},{320,384},{384,448},... | collective-permute-start | bytes 626696 | tf_op jit(solution)/shard_map/ppermute | solution.py:345
  45.0 10.5 %all-to-all-start.1 = ((f32[64,1,128]{2,1,0:T(1,128)}), f32[64,1,128]{2,1,0:T(1,128)S(1)}, u32[]{:S(2)}, u32[]{:S(2)}) async-start(f32[64,1,128]{2,1,0:T(1,128)} %get-tuple-element.32), calls=%async_computation.1 | async-start | bytes 65536 | tf_op jit(solution)/shard_map/all_to_all | solution.py:389
  55.6 2.7 %collective-permute-start.1 = (f32[408,128]{1,0:T(8,128)S(1)}, f32[408,128]{1,0:T(8,128)S(1)}, u32[]{:S(2)}, u32[]{:S(2)}) collective-permute-start(f32[408,128]{1,0:T(8,128)S(1)} %get-tuple-element.25), channel_id=1, source_target_pairs={{0,960},{64,0},{128,64},{192,128},{256,192},{320,256},{384,320},{4... | collective-permute-start | bytes 626696 | tf_op jit(solution)/shard_map/ppermute | solution.py:345
  58.2 0.0 collective-permute-done.refs_5_
  58.3 26.1 %collective-permute-done.1.refs_6_ = f32[408,128]{1,0:T(8,128)S(1)} collective-permute-done((f32[408,128]{1,0:T(8,128)S(1)}, f32[408,128]{1,0:T(8,128)S(1)}, u32[]{:S(2)}, u32[]{:S(2)}) %collective-permute-start.1) | collective-permute-done | bytes 208928 | tf_op jit(solution)/shard_map/ppermute | solution.py:345
  84.3 0.0 collective-permute-start.2
  84.4 2.9 %collective-permute-start.3 = (f32[40,128]{1,0:T(8,128)S(1)}, f32[40,128]{1,0:T(8,128)S(1)}, u32[]{:S(2)}, u32[]{:S(2)}) collective-permute-start(f32[40,128]{1,0:T(8,128)S(1)} %pad_maximum_fusion.1), channel_id=1, source_target_pairs={{0,60},{4,0},{8,4},{12,8},{16,12},{20,16},{24,20},{28,24},{32,28},... | collective-permute-start | bytes 61448 | tf_op jit(solution)/shard_map/ppermute | solution.py:345
  87.3 0.1 reshape.24.refs_2_
  87.4 0.0 copy-done.7
  87.4 0.2 copy.15
  87.6 0.1 reshape.22.refs_0_
  87.7 0.2 copy.16
  87.9 0.1 reshape.23.refs_1_
  88.0 0.0 all-to-all-done.1
  88.0 0.1 reduce_max.18
  88.1 0.1 reshape.25
  88.2 16.6 %pmax.7 = f32[2,64]{1,0:T(2,128)S(1)} all-reduce(f32[2,64]{1,0:T(2,128)S(1)} %reshape.25), channel_id=1, replica_groups=mesh['face_0'=4,'face_1'=4,'tile_0'=8,'tile_1'=2,'lev'=4] {'face_0'}, use_global_device_ids=true, to_apply=%region_1.0 | all-reduce | flops 128 | bytes 1024 | tf_op jit(solution)/shard_map/pmax | solution.py:390
  104.8 0.6 reduce_max.19
  105.5 0.0 collective-permute-done.2.refs_7_
  105.5 0.0 collective-permute-done.3.refs_8_
  105.5 5.5 %sum.1 = (f32[2,18,8,128]{3,2,1,0:T(8,128)}, f32[18,8,128]{2,1,0:T(8,128)}, f32[18,8,128]{2,1,0:T(8,128)}, f32[18,18,8,128]{3,2,1,0:T(8,128)}) custom-call(s32[512]{0:T(512)S(1)} %reshape.22.refs_0_, s32[512]{0:T(512)S(1)} %reshape.23.refs_1_, s32[256]{0:T(256)S(1)} %reshape.24.refs_2_, f32[3200,128]{1,0:T(8,128)S(1)} %get-tuple-element.19.refs_1_.refs_3_, ...), custom_call_target="tpu_custom_call" | custom-call | tf_op jit(solution)/shard_map/sum/pallas_call | solution.py:397
  (15 shorter events, 0.0 us)
Async XLA Ops:
  0.6 1.3 %copy-start = (f32[18,18,8,128]{3,2,1,0:T(8,128)S(1)}, f32[18,18,8,128]{3,2,1,0:T(8,128)}, u32[]{:S(2)}) copy-start(f32[18,18,8,128]{3,2,1,0:T(8,128)} %refs_3_.1) | copy-start | bytes 3981316
  2.0 0.9 copy-start.1
  2.9 0.9 copy-start.2
  3.8 0.9 copy-start.3
  4.6 0.7 copy-start.4
  5.4 0.7 copy-start.5
  6.0 0.7 copy-start.6
  20.5 66.8 %copy-start.9 = (s32[16,16]{1,0:T(8,128)S(1)}, s32[16,16]{1,0:T(8,128)}, u32[]{:S(2)}) copy-start(s32[16,16]{1,0:T(8,128)} %param.19) | copy-start | bytes 3076
  20.5 66.9 %copy-start.7 = (s32[16,16,2]{1,2,0:T(2,128)S(1)}, s32[16,16,2]{1,2,0:T(2,128)}, u32[]{:S(2)}) copy-start(s32[16,16,2]{1,2,0:T(2,128)} %param.17) | copy-start | bytes 6148
  20.5 67.2 %copy-start.8 = (s32[16,16,2]{1,2,0:T(2,128)S(1)}, s32[16,16,2]{1,2,0:T(2,128)}, u32[]{:S(2)}) copy-start(s32[16,16,2]{1,2,0:T(2,128)} %param.18) | copy-start | bytes 6148
  34.2 24.1 %collective-permute-start = (f32[408,128]{1,0:T(8,128)S(1)}, f32[408,128]{1,0:T(8,128)S(1)}, u32[]{:S(2)}, u32[]{:S(2)}) collective-permute-start(f32[408,128]{1,0:T(8,128)S(1)} %get-tuple-element.24), channel_id=1, source_target_pairs={{0,64},{64,128},{128,192},{192,256},{256,320},{320,384},{384,448},... | collective-permute-start | bytes 626696 | tf_op jit(solution)/shard_map/ppermute | solution.py:345
  45.0 43.0 %all-to-all-start.1 = ((f32[64,1,128]{2,1,0:T(1,128)}), f32[64,1,128]{2,1,0:T(1,128)S(1)}, u32[]{:S(2)}, u32[]{:S(2)}) async-start(f32[64,1,128]{2,1,0:T(1,128)} %get-tuple-element.32), calls=%async_computation.1 | async-start | bytes 65536 | tf_op jit(solution)/shard_map/all_to_all | solution.py:389
  55.6 28.7 %collective-permute-start.1 = (f32[408,128]{1,0:T(8,128)S(1)}, f32[408,128]{1,0:T(8,128)S(1)}, u32[]{:S(2)}, u32[]{:S(2)}) collective-permute-start(f32[408,128]{1,0:T(8,128)S(1)} %get-tuple-element.25), channel_id=1, source_target_pairs={{0,960},{64,0},{128,64},{192,128},{256,192},{320,256},{384,320},{4... | collective-permute-start | bytes 626696 | tf_op jit(solution)/shard_map/ppermute | solution.py:345
  84.3 21.1 %collective-permute-start.2 = (f32[40,128]{1,0:T(8,128)S(1)}, f32[40,128]{1,0:T(8,128)S(1)}, u32[]{:S(2)}, u32[]{:S(2)}) collective-permute-start(f32[40,128]{1,0:T(8,128)S(1)} %pad_maximum_fusion), channel_id=1, source_target_pairs={{0,4},{4,8},{8,12},{12,16},{16,20},{20,24},{24,28},{28,32},{32,36}... | collective-permute-start | bytes 61448 | tf_op jit(solution)/shard_map/ppermute | solution.py:345
  84.4 21.1 %collective-permute-start.3 = (f32[40,128]{1,0:T(8,128)S(1)}, f32[40,128]{1,0:T(8,128)S(1)}, u32[]{:S(2)}, u32[]{:S(2)}) collective-permute-start(f32[40,128]{1,0:T(8,128)S(1)} %pad_maximum_fusion.1), channel_id=1, source_target_pairs={{0,60},{4,0},{8,4},{12,8},{16,12},{20,16},{24,20},{28,24},{32,28},... | collective-permute-start | bytes 61448 | tf_op jit(solution)/shard_map/ppermute | solution.py:345
